TPU v7x, 32 devices: a whole 2x2x4 slice. The times are simulated.
32 devices in a mesh: paths: 4 (over y, core), contract: 8 (over z, x).
Axes of the slice: x: 2, y: 2, z: 4, core: 2. Of those that a mesh axis runs over, the one named last changes fastest.
Arguments:
- prices: float32 [1, 512], P(None, 'paths'), may hold values from -6 to 6
- terminal: bfloat16 [128, 512, 128], P('contract', 'paths'), may hold values from -6 to 6
- band: int32 [128], replicated, may hold values from 32 to 128
- position: int32 [128], replicated, may hold values from 0 to 127, as said below
- actions: int32 [128, 3], replicated, may hold values from -3 to 3
- degree: int32 [128], replicated, may hold values from 2 to 7
- volume: float32 [128], replicated, may hold values from 0.05 to 0.5
Outputs:
- valued: bfloat16 [128, 512, 128], P('contract', 'paths')
Inputs may be any that keep to these rules, and one draw needn't show every extreme that they name: A permutation of the contracts; contract c goes to new block position[c] // 16. Each old block of 16 contracts sends exactly 2 contracts to each of the 8 new blocks.
All inputs are finite; a program needn't handle non-finite values.
Results may differ from a plain program's by a relative error of at most 0.0038.
Values may be sent and summed in bfloat16 or wider, within the bound.
No kernel may reach another device: no remote copies, remote signals or barrier semaphores. Data moves between devices by JAX's collectives and lax.ppermute only.
A program may use at most 64 MiB of HBM per device.

v0:
```python
import jax
import jax.numpy as jnp
from jax import lax
from jax.sharding import PartitionSpec as P

LEVELS = 128
BASIS = 8
MOVE = 3
RIDGE = 0.05
DISCOUNT = 0.98
SPOT_SCALE = 0.25


def chebyshev(prices_row):
    scaled = jnp.tanh(prices_row)
    series = [jnp.ones_like(scaled), scaled]
    for order in range(2, BASIS):
        series.append(2.0 * scaled * series[-1] - series[-2])
    return jnp.stack(series[:BASIS])


def regress(gram, moments, path_count, degree_block):
    orders = jnp.arange(BASIS, dtype=jnp.int32)
    keep_basis = (orders[None, :] <= degree_block[:, None]).astype(jnp.float32)
    identity = jnp.eye(BASIS, dtype=jnp.float32)
    system = keep_basis[:, :, None] * keep_basis[:, None, :] * (gram / path_count)[None]
    system = system + (1.0 - keep_basis)[:, :, None] * identity[None] + RIDGE * identity[None]
    scaled_moments = keep_basis[:, :, None] * (moments / path_count)
    factor = jnp.linalg.cholesky(system)
    halfway = lax.linalg.triangular_solve(factor, scaled_moments, left_side=True, lower=True)
    return lax.linalg.triangular_solve(
        factor, halfway, left_side=True, lower=True, transpose_a=True
    )


def decide(values_now, estimate, spot_price, band_block, action_block, volume_block):
    levels = jnp.arange(LEVELS, dtype=jnp.int32)
    living = levels[None, :] < band_block[:, None]
    padded = jnp.pad(estimate, ((0, 0), (0, 0), (MOVE, MOVE)))
    optimum = DISCOUNT * estimate
    for offset in range(-MOVE, MOVE + 1):
        if offset == 0:
            continue
        allowed = jnp.any(action_block == offset, axis=1)
        target_level = levels + offset
        inside = (target_level[None, :] >= 0) & (target_level[None, :] < band_block[:, None])
        moved = padded[:, :, MOVE + offset : MOVE + offset + LEVELS]
        candidate = (
            -offset * volume_block[:, None, None] * spot_price[None, :, None] + DISCOUNT * moved
        )
        usable = allowed[:, None, None] & inside[:, None, :]
        optimum = jnp.where(usable, jnp.maximum(optimum, candidate), optimum)
    return jnp.where(living[:, None, :], optimum + DISCOUNT * (values_now - estimate), 0.0)


def lookup_flat(contract_ids, table):
    matches = contract_ids[:, None] == jnp.arange(table.shape[0], dtype=jnp.int32)[None, :]
    return jnp.sum(jnp.where(matches, table[None, :], jnp.zeros((), table.dtype)), axis=1)


def lookup_rows(contract_ids, table):
    matches = contract_ids[:, None] == jnp.arange(table.shape[0], dtype=jnp.int32)[None, :]
    return jnp.sum(
        jnp.where(matches[:, :, None], table[None, :, :], jnp.zeros((), table.dtype)), axis=1
    )


def redistribute(grids, position, block_count, myself, capacity):
    con_count = grids.shape[0]
    slot_ids = jnp.arange(con_count, dtype=jnp.int32)
    target = position // con_count
    target_grid = target.reshape(block_count, con_count)
    mine = lax.dynamic_slice_in_dim(target, myself * con_count, con_count)
    earlier = slot_ids[None, :] < slot_ids[:, None]
    rank_out = jnp.sum(earlier & (mine[None, :] == mine[:, None]), axis=1)
    flat_slot = mine * capacity + rank_out
    send_slots = jnp.arange(block_count * capacity, dtype=jnp.int32)
    matches = flat_slot[None, :] == send_slots[:, None]
    source_row = jnp.sum(jnp.where(matches, slot_ids[None, :], 0), axis=1)
    filled = jnp.any(matches, axis=1)
    outgoing = jnp.where(filled[:, None, None], grids[source_row], jnp.zeros((), grids.dtype))
    outgoing = outgoing.reshape((block_count, capacity) + grids.shape[1:])
    incoming = lax.all_to_all(outgoing, "contract", split_axis=0, concat_axis=0, tiled=True)
    wanted = myself * con_count + slot_ids
    owner_match = position[None, :] == wanted[:, None]
    owner_ids = jnp.sum(
        jnp.where(owner_match, jnp.arange(position.shape[0], dtype=jnp.int32)[None, :], 0), axis=1
    )
    source_block = owner_ids // con_count
    source_slot = owner_ids % con_count
    block_match = source_block[:, None] == jnp.arange(block_count, dtype=jnp.int32)[None, :]
    peer_targets = jnp.sum(jnp.where(block_match[:, :, None], target_grid[None, :, :], 0), axis=1)
    rank_in = jnp.sum((slot_ids[None, :] < source_slot[:, None]) & (peer_targets == myself), axis=1)
    chosen = source_block * capacity + rank_in
    arrived = incoming.reshape((block_count * capacity,) + grids.shape[1:])[chosen]
    return (arrived, owner_ids)


def window(prices, values_now, contract_ids, band, actions, degree, volume, path_count):
    highest = lax.Precision.HIGHEST
    band_block = lookup_flat(contract_ids, band)
    degree_block = lookup_flat(contract_ids, degree)
    volume_block = lookup_flat(contract_ids, volume)
    action_block = lookup_rows(contract_ids, actions)
    basis_rows = chebyshev(prices[0])
    spot_price = jnp.exp(SPOT_SCALE * prices[0])
    gram_part = jnp.dot(basis_rows, basis_rows.T, precision=highest)
    moments = jnp.einsum("kp,cpl->ckl", basis_rows, values_now, precision=highest)
    gram = lax.psum(gram_part.astype(jnp.bfloat16), "paths").astype(jnp.float32)
    moments_all = lax.psum(moments.astype(jnp.bfloat16), "paths").astype(jnp.float32)
    fitted = regress(gram, moments_all, path_count, degree_block)
    estimate = jnp.einsum("kp,ckl->cpl", basis_rows, fitted, precision=highest)
    values_now = decide(values_now, estimate, spot_price, band_block, action_block, volume_block)
    return values_now


def per_device(prices, terminal, band, position, actions, degree, volume):
    block_count = lax.axis_size("contract")
    myself = lax.axis_index("contract")
    con_count = terminal.shape[0]
    capacity = con_count // block_count
    path_count = prices.shape[1] * lax.axis_size("paths")
    grids, contract_ids = redistribute(terminal, position, block_count, myself, capacity)
    values_now = window(
        prices, grids.astype(jnp.float32), contract_ids, band, actions, degree, volume, path_count
    )
    result = values_now.astype(jnp.bfloat16)
    return result


def solution(mesh):
    in_specs = (P(None, "paths"), P("contract", "paths", None), P(), P(), P(), P(), P())
    out_specs = P("contract", "paths", None)
    return jax.shard_map(
        per_device, mesh=mesh, in_specs=in_specs, out_specs=out_specs, check_vma=False
    )
```

profile of v0, /device:TPU:0, one launch (start us, length us, event | category | flops | bytes accessed | tf_op | source)
XLA Modules:
  0.0 64.9 jit_solution(13784414937052553500)
XLA Ops:
  0.0 0.0 copy-start
  0.0 0.7 %and_select_fusion.3 = s32[128]{0:T(128)S(1)} fusion(s32[128]{0:T(128)} %param.10), kind=kLoop, calls=%fused_computation.97 | loop fusion | flops 1920 | bytes 1024 | tf_op jit(solution)/shard_map/jit(floor_divide)/jit(_where)/select_n | solution.py:71
  0.7 0.1 dynamic_slice.3
  0.8 0.2 convert_reduce_fusion.1
  1.0 0.1 multiply_add_fusion
  1.1 0.1 select_reduce_fusion.4
  1.2 0.1 fusion.25
  1.3 0.1 broadcast_in_dim.162
  1.4 0.6 gather_fusion
  2.1 0.0 copy-start.5
  2.1 0.0 copy-start.6
  2.1 0.0 copy-start.1
  2.1 0.0 copy-start.2
  2.1 0.0 copy-start.3
  2.1 0.0 copy-start.4
  2.1 0.9 %broadcast_select_fusion = bf16[8,2,128,128]{3,2,1,0:T(8,128)(2,1)} fusion(bf16[8,2,128,128]{3,2,1,0:T(8,128)(2,1)S(1)} %bitcast.48, pred[8,2]{1,0:T(8,128)(4,1)S(1)} %broadcast_in_dim.162), kind=kLoop, calls=%fused_computation.27 | loop fusion | flops 262144 | bytes 1048592 | tf_op jit(solution)/shard_map/jit(_where)/select_n | solution.py:81
  3.0 7.3 %all-to-all-start = ((bf16[8,2,128,128]{3,2,1,0:T(8,128)(2,1)}), bf16[8,2,128,128]{3,2,1,0:T(8,128)(2,1)S(1)}, u32[]{:S(2)}, u32[]{:S(2)}) async-start(bf16[8,2,128,128]{3,2,1,0:T(8,128)(2,1)} %broadcast_select_fusion), calls=%async_computation | async-start | bytes 1048576 | tf_op jit(solution)/shard_map/all_to_all | solution.py:83
  10.4 0.2 select_reduce_fusion.7
  10.6 0.1 iota_compare_fusion.5
  10.7 0.1 broadcast_in_dim.167
  10.8 0.2 select_reduce_fusion.3
  11.0 0.1 iota_compare_fusion
  11.1 0.1 select_reduce_fusion.2
  11.3 0.1 select_reduce_fusion
  11.4 0.2 convert_reduce_fusion
  11.6 0.2 select_reduce_fusion.6
  11.8 0.1 fusion.27
  11.9 0.1 convolution_convert_fusion.1
  12.1 0.1 fusion.26
  12.1 0.1 iota_compare_fusion.6
  12.2 0.1 broadcast_multiply_fusion.5
  12.3 12.5 %all-to-all-done = bf16[8,2,128,128]{3,2,1,0:T(8,128)(2,1)S(1)} async-done(((bf16[8,2,128,128]{3,2,1,0:T(8,128)(2,1)}), bf16[8,2,128,128]{3,2,1,0:T(8,128)(2,1)S(1)}, u32[]{:S(2)}, u32[]{:S(2)}) %all-to-all-start) | async-done | bytes 524320 | tf_op jit(solution)/shard_map/all_to_all | solution.py:83
  24.8 0.6 gather_fusion.1
  25.5 0.3 fusion
  25.8 0.3 copy.28
  26.1 10.5 %all-reduce.1 = (bf16[8,8]{1,0:T(8,128)(2,1)S(1)}, bf16[16,8,128]{2,1,0:T(8,128)(2,1)S(1)}) all-reduce(bf16[8,8]{1,0:T(8,128)(2,1)S(1)} %convolution_convert_fusion.1, bf16[16,8,128]{2,1,0:T(8,128)(2,1)S(1)} %fusion), channel_id=1, replica_groups=mesh['paths'=4,'contract'=8] {'paths'}, use_global_device_ids=true, to_apply=%region_10.11 | all-reduce | flops 16448 | bytes 65792 | tf_op jit(solution)/shard_map/psum | solution.py:109
  36.6 0.1 copy.24
  36.6 0.1 fusion.15
  36.8 11.7 %custom-call.9 = f32[16,8,8]{2,1,0:T(8,128)S(1)} custom-call(f32[16,8,8]{2,1,0:T(8,128)S(1)} %fusion.15), custom_call_target="Cholesky" | custom-call | tf_op jit(solution)/shard_map/jit(cholesky)/cholesky | solution.py:29
  48.5 0.1 select_reduce_fusion.1
  48.6 0.1 copy.25
  48.6 0.1 select_bitcast_fusion
  48.7 10.0 %custom-call.10 = f32[16,1,8,8]{2,3,1,0:T(8,128)S(1)} custom-call(f32[16,1,8,8]{3,2,1,0:T(8,128)S(1)} %select_bitcast_fusion), custom_call_target="InvertDiagBlocksLowerTriangular" | custom-call | tf_op jit(solution)/shard_map/triangular_solve | solution.py:31
  58.8 0.4 fusion.20
  59.2 0.3 fusion.18
  59.4 1.8 %convolution_bitcast_fusion = f32[16,128,128]{1,2,0:T(8,128)S(1)} fusion(f32[16,8,128]{2,1,0:T(8,128)S(1)} %fusion.18, f32[8,128]{1,0:T(8,128)S(1)} %stack.2), kind=kOutput, calls=%fused_computation.8 | convolution fusion | flops 25165824 | bytes 1118208 | tf_op jit(solution)/shard_map/kp,ckl->cpl/dot_general | solution.py:112
  61.3 2.6 %fusion.11 = bf16[16,128,128]{1,2,0:T(8,128)(2,1)S(1)} fusion(f32[16,128,128]{1,2,0:T(8,128)S(1)} %convolution_bitcast_fusion, bf16[16,128,128]{1,2,0:T(8,128)(2,1)S(1)} %copy.28, f32[16,128]{1,0:T(8,128)S(1)} %get-tuple-element.34, f32[16,128]{1,0:T(8,128)S(1)} %get-tuple-element.33, f32[16,128]{1,0:T(8,128)S(1)} %get-tuple-element.32, ...), kind=kLoop, calls=%fused_computation.26 | loop fusion | flops 8126464 | bytes 2160640 | tf_op jit(solution)/shard_map/convert_element_type | solution.py:127
  63.9 1.0 %copy.29 = bf16[16,128,128]{2,1,0:T(8,128)(2,1)} copy(bf16[16,128,128]{1,2,0:T(8,128)(2,1)S(1)} %fusion.11) | data formatting | bytes 1048576 | tf_op jit(solution)/shard_map/convert_element_type | solution.py:127
  (31 shorter events, 0.2 us)
Async XLA Ops:
  0.0 1.4 %copy-start = (bf16[16,128,128]{2,1,0:T(8,128)(2,1)S(1)}, bf16[16,128,128]{2,1,0:T(8,128)(2,1)}, u32[]{:S(2)}) copy-start(bf16[16,128,128]{2,1,0:T(8,128)(2,1)} %param.8) | copy-start | bytes 1572868
  2.1 8.3 %copy-start.5 = (s32[128]{0:T(128)S(1)}, s32[128]{0:T(128)}, u32[]{:S(2)}) copy-start(s32[128]{0:T(128)} %param.10) | copy-start | bytes 1540
  2.1 8.7 %copy-start.6 = (f32[128]{0:T(128)S(1)}, f32[128]{0:T(128)}, u32[]{:S(2)}) copy-start(f32[128]{0:T(128)} %param.13) | copy-start | bytes 1540
  2.1 9.0 %copy-start.1 = (s32[128,3]{0,1:T(4,128)S(1)}, s32[128,3]{0,1:T(4,128)}, u32[]{:S(2)}) copy-start(s32[128,3]{0,1:T(4,128)} %param.11) | copy-start | bytes 4612
  2.1 9.1 %copy-start.2 = (f32[1,128]{1,0:T(1,128)S(1)}, f32[1,128]{1,0:T(1,128)}, u32[]{:S(2)}) copy-start(f32[1,128]{1,0:T(1,128)} %param.7) | copy-start | bytes 1540
  2.1 9.5 %copy-start.3 = (s32[128]{0:T(128)S(1)}, s32[128]{0:T(128)}, u32[]{:S(2)}) copy-start(s32[128]{0:T(128)} %param.9) | copy-start | bytes 1540
  2.1 9.5 %copy-start.4 = (s32[128]{0:T(128)S(1)}, s32[128]{0:T(128)}, u32[]{:S(2)}) copy-start(s32[128]{0:T(128)} %param.12) | copy-start | bytes 1540
  3.0 21.8 %all-to-all-start = ((bf16[8,2,128,128]{3,2,1,0:T(8,128)(2,1)}), bf16[8,2,128,128]{3,2,1,0:T(8,128)(2,1)S(1)}, u32[]{:S(2)}, u32[]{:S(2)}) async-start(bf16[8,2,128,128]{3,2,1,0:T(8,128)(2,1)} %broadcast_select_fusion), calls=%async_computation | async-start | bytes 1048576 | tf_op jit(solution)/shard_map/all_to_all | solution.py:83
where the time goes:
time: 65.1 us; the launch traced here: 64.9 us
  other arithmetic  28.4 us (44%)
  waiting for transfers between devices  12.5 us (19%)
  blocking collectives  10.5 us (16%)
  starting transfers between devices  7.28 us (11%)
  local copies, waits for them, and re-layouts  3.04 us (5%)
  matrix products  2.92 us (4%)
    all_to_all x1, waiting for transfers between devices, redistribute(): lax.all_to_all(outgoing, 'contract', split_axis=0, concat_axis=0, tiled=T...  12.5 us
    another operation x4, other arithmetic, regress(): factor = jnp.linalg.cholesky(system)  11.8 us
    psum x1, blocking collectives, window(): gram = lax.psum(gram_part.astype(jnp.bfloat16), 'paths').astype(jnp.float32)  10.5 us
    another operation x3, other arithmetic, regress(): lax.linalg.triangular_solve(factor, halfway, left_side=True, lower=True,...  10.1 us
    all_to_all x1, starting transfers between devices, redistribute(): lax.all_to_all(outgoing, 'contract', split_axis=0, concat_axis=0, tiled=T...  7.28 us
    convert_element_type x1, other arithmetic, per_device(): result = values_now.astype(jnp.bfloat16)  2.63 us
    dot_general x1, matrix products, window(): estimate = jnp.einsum('kp,ckl->cpl', basis_rows, fitted, precision=highest)  1.81 us
  transfers between devices with their start and end apart: 1, of which 1 were waited for; matrix products, arithmetic and copies ran while one was open for 3% of the time, Pallas kernels for 0%

commit v1 on v0

--- a/solution.py
+++ b/solution.py
@@ -106,7 +106,9 @@
     spot_price = jnp.exp(SPOT_SCALE * prices[0])
     gram_part = jnp.dot(basis_rows, basis_rows.T, precision=highest)
     moments = jnp.einsum("kp,cpl->ckl", basis_rows, values_now, precision=highest)
-    gram = lax.psum(gram_part.astype(jnp.bfloat16), "paths").astype(jnp.float32)
+    gram = jnp.sum(lax.all_gather(gram_part.astype(jnp.bfloat16), "paths"), axis=0).astype(
+        jnp.float32
+    )
     moments_all = lax.psum(moments.astype(jnp.bfloat16), "paths").astype(jnp.float32)
     fitted = regress(gram, moments_all, path_count, degree_block)
     estimate = jnp.einsum("kp,ckl->cpl", basis_rows, fitted, precision=highest)

time: 65.1 us -> 59.1 us (0.908)
  waiting for transfers between devices: 12.5 us -> 0.01 us
  blocking collectives: 10.5 us -> 16.8 us
    all_to_all x1, waiting for transfers between devices: 12.5 us -> 0.01 us  [redistribute(): lax.all_to_all(outgoing, 'contract', split_axis=0, concat_axis=0, tiled=T...]
    all_gather x0 -> x1, blocking collectives: none -> 5.19 us  [window(): lax.all_gather(gram_part.astype(jnp.bfloat16), 'paths')]
    psum x1, blocking collectives: 10.5 us -> 11.6 us  [window(): lax.psum(moments.astype(jnp.bfloat16), 'paths').astype(jnp.float32)]
  transfers between devices with their start and end apart: 1 -> 1, of which waited for: 1 -> 0; matrix products, arithmetic and copies ran while one was open for 3% -> 41% of each run, Pallas kernels for 0% -> 0%
where the time goes in v1:
time: 59.1 us; the launch traced here: 58.9 us
  other arithmetic  28.4 us (48%)
  blocking collectives  16.8 us (28%)
  starting transfers between devices  7.41 us (13%)
  local copies, waits for them, and re-layouts  3.04 us (5%)
  matrix products  2.84 us (5%)
    another operation x4, other arithmetic, regress(): factor = jnp.linalg.cholesky(system)  11.8 us
    psum x1, blocking collectives, window(): lax.psum(moments.astype(jnp.bfloat16), 'paths').astype(jnp.float32)  11.6 us
    another operation x3, other arithmetic, regress(): lax.linalg.triangular_solve(factor, halfway, left_side=True, lower=True,...  10.1 us
    all_to_all x1, starting transfers between devices, redistribute(): lax.all_to_all(outgoing, 'contract', split_axis=0, concat_axis=0, tiled=T...  7.41 us
    all_gather x1, blocking collectives, window(): lax.all_gather(gram_part.astype(jnp.bfloat16), 'paths')  5.19 us
    convert_element_type x1, other arithmetic, per_device(): result = values_now.astype(jnp.bfloat16)  2.62 us
    dot_general x1, matrix products, window(): estimate = jnp.einsum('kp,ckl->cpl', basis_rows, fitted, precision=highest)  1.81 us
  transfers between devices with their start and end apart: 1, of which 0 were waited for; matrix products, arithmetic and copies ran while one was open for 41% of the time, Pallas kernels for 0%

profile of v1, /device:TPU:0, one launch (start us, length us, event | category | flops | bytes accessed | tf_op | source)
XLA Modules:
  0.0 58.9 jit_solution(2211462672738641033)
XLA Ops:
  0.0 0.7 %and_select_fusion.3 = s32[128]{0:T(128)S(1)} fusion(s32[128]{0:T(128)} %param.10), kind=kLoop, calls=%fused_computation.98 | loop fusion | flops 1920 | bytes 1024 | tf_op jit(solution)/shard_map/jit(floor_divide)/jit(_where)/select_n | solution.py:71
  0.7 0.1 dynamic_slice.3
  0.8 0.2 convert_reduce_fusion.1
  1.0 0.1 multiply_add_fusion
  1.1 0.1 select_reduce_fusion.4
  1.2 0.1 fusion.25
  1.3 0.1 broadcast_in_dim.162
  1.4 0.6 %gather_fusion = bf16[16,128,128]{2,1,0:T(8,128)(2,1)S(1)} fusion(bf16[16,128,128]{2,1,0:T(8,128)(2,1)S(1)} %copy-done, s32[1024]{0:T(1024)S(1)} %pad_clamp_fusion.1), kind=kCustom, calls=%fused_computation | custom fusion | bytes 1048640 | tf_op jit(solution)/shard_map/gather | solution.py:81
  2.1 0.0 copy-start.5
  2.1 0.0 copy-start.3
  2.1 0.0 copy-start.4
  2.1 0.0 copy-start.2
  2.1 0.0 copy-start.1
  2.1 0.9 %broadcast_select_fusion = bf16[8,2,128,128]{3,2,1,0:T(8,128)(2,1)} fusion(bf16[8,2,128,128]{3,2,1,0:T(8,128)(2,1)S(1)} %bitcast.50, pred[8,2]{1,0:T(8,128)(4,1)S(1)} %broadcast_in_dim.162), kind=kLoop, calls=%fused_computation.27 | loop fusion | flops 262144 | bytes 1048592 | tf_op jit(solution)/shard_map/jit(_where)/select_n | solution.py:81
  3.0 7.4 %all-to-all-start = ((bf16[8,2,128,128]{3,2,1,0:T(8,128)(2,1)}), bf16[8,2,128,128]{3,2,1,0:T(8,128)(2,1)S(1)}, u32[]{:S(2)}, u32[]{:S(2)}) async-start(bf16[8,2,128,128]{3,2,1,0:T(8,128)(2,1)} %broadcast_select_fusion), calls=%async_computation | async-start | bytes 1048576 | tf_op jit(solution)/shard_map/all_to_all | solution.py:83
  10.5 0.2 select_reduce_fusion.7
  10.7 0.1 iota_compare_fusion.5
  10.8 0.1 broadcast_in_dim.167
  10.9 0.2 select_reduce_fusion.6
  11.1 0.1 fusion.27
  11.2 0.1 fusion.26
  11.3 0.1 iota_compare_fusion
  11.4 0.1 convolution_convert_fusion.1
  11.5 0.1 select_reduce_fusion
  11.7 0.2 convert_reduce_fusion
  11.9 5.2 %all-gather = bf16[32,8]{1,0:T(8,128)(2,1)S(1)} all-gather(bf16[8,8]{1,0:T(8,128)(2,1)S(1)} %convolution_convert_fusion.1), channel_id=2, replica_groups=mesh['paths'=4,'contract'=8] {'paths'}, dimensions={0}, use_global_device_ids=true | all-gather | bytes 640 | tf_op jit(solution)/shard_map/all_gather | solution.py:109
  17.1 0.1 copy.29
  17.2 0.1 fusion.15
  17.3 11.7 %custom-call.9 = f32[16,8,8]{2,1,0:T(8,128)S(1)} custom-call(f32[16,8,8]{2,1,0:T(8,128)S(1)} %fusion.15), custom_call_target="Cholesky" | custom-call | tf_op jit(solution)/shard_map/jit(cholesky)/cholesky | solution.py:29
  29.0 0.1 select_reduce_fusion.1
  29.1 0.1 copy.30
  29.2 0.1 select_reduce_fusion.2
  29.3 0.1 select_bitcast_fusion
  29.4 10.0 %custom-call.10 = f32[16,1,8,8]{2,3,1,0:T(8,128)S(1)} custom-call(f32[16,1,8,8]{3,2,1,0:T(8,128)S(1)} %select_bitcast_fusion), custom_call_target="InvertDiagBlocksLowerTriangular" | custom-call | tf_op jit(solution)/shard_map/triangular_solve | solution.py:31
  39.4 0.1 compare_reduce_fusion.6
  39.5 0.2 select_reduce_fusion.3
  39.7 0.1 iota_compare_fusion.6
  39.8 0.1 broadcast_multiply_fusion.5
  39.9 0.0 all-to-all-done
  39.9 0.6 %gather_fusion.1 = bf16[16,128,128]{2,1,0:T(8,128)(2,1)S(1)} fusion(bf16[16,128,128]{2,1,0:T(8,128)(2,1)S(1)} %bitcast.49, s32[1024]{0:T(1024)S(1)} %pad_clamp_fusion), kind=kCustom, calls=%fused_computation.1 | custom fusion | bytes 1048640 | tf_op jit(solution)/shard_map/gather | solution.py:95
  40.6 0.3 fusion
  40.9 0.3 copy.33
  41.2 11.6 %psum.7 = bf16[16,8,128]{2,1,0:T(8,128)(2,1)S(1)} all-reduce(bf16[16,8,128]{2,1,0:T(8,128)(2,1)S(1)} %fusion), channel_id=1, replica_groups=mesh['paths'=4,'contract'=8] {'paths'}, use_global_device_ids=true, to_apply=%region_18.19 | all-reduce | flops 16384 | bytes 65536 | tf_op jit(solution)/shard_map/psum | solution.py:112
  52.8 0.3 fusion.20
  53.2 0.3 fusion.18
  53.4 1.8 %convolution_bitcast_fusion = f32[16,128,128]{1,2,0:T(8,128)S(1)} fusion(f32[16,8,128]{2,1,0:T(8,128)S(1)} %fusion.18, f32[8,128]{1,0:T(8,128)S(1)} %stack.2), kind=kOutput, calls=%fused_computation.8 | convolution fusion | flops 25165824 | bytes 1118208 | tf_op jit(solution)/shard_map/kp,ckl->cpl/dot_general | solution.py:114
  55.2 2.6 %fusion.11 = bf16[16,128,128]{1,2,0:T(8,128)(2,1)S(1)} fusion(f32[16,128,128]{1,2,0:T(8,128)S(1)} %convolution_bitcast_fusion, bf16[16,128,128]{1,2,0:T(8,128)(2,1)S(1)} %copy.33, f32[16,128]{1,0:T(8,128)S(1)} %get-tuple-element.32, f32[16,128]{1,0:T(8,128)S(1)} %get-tuple-element.31, f32[16,128]{1,0:T(8,128)S(1)} %get-tuple-element.30, ...), kind=kLoop, calls=%fused_computation.26 | loop fusion | flops 8126464 | bytes 2160640 | tf_op jit(solution)/shard_map/convert_element_type | solution.py:129
  57.9 1.0 %copy.34 = bf16[16,128,128]{2,1,0:T(8,128)(2,1)} copy(bf16[16,128,128]{1,2,0:T(8,128)(2,1)S(1)} %fusion.11) | data formatting | bytes 1048576 | tf_op jit(solution)/shard_map/convert_element_type | solution.py:129
  (33 shorter events, 0.2 us)
Async XLA Ops:
  0.0 1.4 %copy-start = (bf16[16,128,128]{2,1,0:T(8,128)(2,1)S(1)}, bf16[16,128,128]{2,1,0:T(8,128)(2,1)}, u32[]{:S(2)}) copy-start(bf16[16,128,128]{2,1,0:T(8,128)(2,1)} %param.8) | copy-start | bytes 1572868
  2.1 8.5 %copy-start.5 = (s32[128]{0:T(128)S(1)}, s32[128]{0:T(128)}, u32[]{:S(2)}) copy-start(s32[128]{0:T(128)} %param.10) | copy-start | bytes 1540
  2.1 8.8 %copy-start.3 = (s32[128]{0:T(128)S(1)}, s32[128]{0:T(128)}, u32[]{:S(2)}) copy-start(s32[128]{0:T(128)} %param.9) | copy-start | bytes 1540
  2.1 8.8 %copy-start.4 = (s32[128]{0:T(128)S(1)}, s32[128]{0:T(128)}, u32[]{:S(2)}) copy-start(s32[128]{0:T(128)} %param.12) | copy-start | bytes 1540
  2.1 9.2 %copy-start.2 = (f32[1,128]{1,0:T(1,128)S(1)}, f32[1,128]{1,0:T(1,128)}, u32[]{:S(2)}) copy-start(f32[1,128]{1,0:T(1,128)} %param.7) | copy-start | bytes 1540
  2.1 27.0 %copy-start.1 = (s32[128,3]{0,1:T(4,128)S(1)}, s32[128,3]{0,1:T(4,128)}, u32[]{:S(2)}) copy-start(s32[128,3]{0,1:T(4,128)} %param.11) | copy-start | bytes 4612
  3.0 36.5 %copy-start.6 = (f32[128]{0:T(128)S(1)}, f32[128]{0:T(128)}, u32[]{:S(2)}) copy-start(f32[128]{0:T(128)} %param.13) | copy-start | bytes 1540
  3.0 36.9 %all-to-all-start = ((bf16[8,2,128,128]{3,2,1,0:T(8,128)(2,1)}), bf16[8,2,128,128]{3,2,1,0:T(8,128)(2,1)S(1)}, u32[]{:S(2)}, u32[]{:S(2)}) async-start(bf16[8,2,128,128]{3,2,1,0:T(8,128)(2,1)} %broadcast_select_fusion), calls=%async_computation | async-start | bytes 1048576 | tf_op jit(solution)/shard_map/all_to_all | solution.py:83
